TPU v7x, 32 devices: a whole 2x2x4 slice. The times are simulated.
32 devices in a mesh: head: 4 (over z), outer: 2 (over core), inner: 4 (over y, x).
Axes of the slice: x: 2, y: 2, z: 4, core: 2. Of those that a mesh axis runs over, the one named last changes fastest.
Arguments:
- query: bfloat16 [4096, 8192], P(('outer', 'inner', 'head')), may hold values from -100 to 100
- keys: bfloat16 [4096, 1024], P(('outer', 'inner', 'head')), may hold values from -4.5 to 4.5
- values: bfloat16 [4096, 1024], P(('outer', 'inner', 'head')), may hold values from -6 to 6
- lengths: int32 [8], replicated, may hold values from 1 to 1024, 4096 in all
Outputs:
- attended: bfloat16 [4096, 8192], P(('outer', 'inner', 'head'))
Inputs may be any that keep to these rules, and one draw needn't show every extreme that they name: `lengths`: they sum to 4096, and the longest is exactly 1024.
All inputs are finite; a program needn't handle non-finite values.
Results may differ from a plain program's by a relative error of at most 0.0038.
Values may be sent and summed in bfloat16 or wider, within the bound.
A program may use at most 64 MiB of HBM per device.

v0:
```python
import functools
import math

import jax
import jax.numpy as jnp
from jax import lax
from jax.experimental import pallas as pl
from jax.experimental.pallas import tpu as pltpu
from jax.sharding import PartitionSpec as P

HEAD_SIZE = 128
MESH = pl.DeviceIdType.MESH


def kernel(
    heads, outers, inners, lengths_ref, q_ref, k_ref, v_ref, out_ref,
    kv, bias, own_sem, z_send, z_recv, y_send, y_recv, x_send, x_recv,
):
    tokens = q_ref.shape[0]
    groups = k_ref.shape[1] // HEAD_SIZE
    width = q_ref.shape[1] // k_ref.shape[1]
    block = heads * tokens
    contexts = outers * inners
    span = (2 * heads + 1) * tokens
    me = lax.axis_index("head")
    ctx = lax.axis_index("outer") * inners + lax.axis_index("inner")
    odd = lax.rem(ctx, 2)

    def context(steps):
        at = lax.rem(ctx + steps + contexts, contexts)
        return {"outer": at // inners, "inner": lax.rem(at, inners)}

    partner = context(1 - 2 * odd)

    def own_copy(g, which):
        ref = (k_ref, v_ref)[which]
        return pltpu.make_async_copy(
            ref.at[:, pl.ds(pl.multiple_of(g * HEAD_SIZE, HEAD_SIZE), HEAD_SIZE)],
            kv.at[g, which, pl.ds(pl.multiple_of(2 * block + me * tokens, tokens), tokens), :],
            own_sem.at[which, g],
        )

    def z_copy(g, shard, way):
        rows = pl.ds(pl.multiple_of(2 * block + shard * tokens, tokens), tokens)
        slot = jnp.where((way < 0) & (shard == me), heads, shard)
        return pltpu.make_async_remote_copy(
            src_ref=kv.at[g, :, rows, :],
            dst_ref=kv.at[g, :, rows, :],
            send_sem=z_send.at[slot, g],
            recv_sem=z_recv.at[shard, g],
            device_id={"head": lax.rem(me + way + heads, heads)},
            device_id_type=MESH,
        )

    def has_next(way):
        return (me + way >= 0) & (me + way < heads)

    def z_onward(g, shard, way):
        @pl.when(has_next(way))
        def _():
            z_copy(g, shard, way).start()

    def z_arrived(g, distance):
        for way in (1, -1):
            shard = me - way * distance

            @pl.when((shard >= 0) & (shard < heads))
            def _():
                z_copy(g, shard, way).wait_recv()
                z_onward(g, shard, way)
                pass_on(g, shard)

    def y_copy(g, shard):
        rows = pl.ds(pl.multiple_of(2 * block + shard * tokens, tokens), tokens)
        landing = pl.ds(pl.multiple_of(shard * tokens, tokens), tokens)
        return pltpu.make_async_remote_copy(
            src_ref=kv.at[g, :, rows, :],
            dst_ref=kv.at[g, :, landing, :],
            send_sem=y_send.at[shard, g],
            recv_sem=y_recv.at[shard, g],
            device_id=context(2),
            device_id_type=MESH,
        )

    def x_copy(g, shard):
        rows = pl.ds(pl.multiple_of((1 - odd) * 2 * block + shard * tokens, tokens), tokens)
        landing = pl.ds(pl.multiple_of(block + shard * tokens, tokens), tokens)
        return pltpu.make_async_remote_copy(
            src_ref=kv.at[g, :, rows, :],
            dst_ref=kv.at[g, :, landing, :],
            send_sem=x_send.at[shard, g],
            recv_sem=x_recv.at[shard, g],
            device_id=partner,
            device_id_type=MESH,
        )

    def y_needed(shard):
        return (odd == 1) | (shard >= me)

    def pass_on(g, shard):
        @pl.when(y_needed(shard))
        def _():
            y_copy(g, shard).start()

        @pl.when(odd == 0)
        def _():
            x_copy(g, shard).start()

    def y_arrived(g, shard):
        @pl.when(y_needed(shard))
        def _():
            y_copy(g, shard).wait_recv()

        @pl.when(odd == 1)
        def _():
            x_copy(g, shard).start()

    for g in range(groups):
        own_copy(g, 0).start()
        own_copy(g, 1).start()

    barrier = pltpu.get_barrier_semaphore()
    for distance in range(1, heads):
        pl.semaphore_signal(
            barrier, inc=1, device_id={"head": lax.rem(me + distance, heads)}, device_id_type=MESH
        )
    for place in (context(2), context(-2), partner):
        pl.semaphore_signal(barrier, inc=1, device_id=place, device_id_type=MESH)
    pl.semaphore_wait(barrier, heads - 1 + 3)

    for g in range(groups):
        own_copy(g, 0).wait()
        own_copy(g, 1).wait()
        z_onward(g, me, 1)
        z_onward(g, me, -1)
        pass_on(g, me)

    first = ctx * block + me * tokens
    query_pos = first + lax.broadcasted_iota(jnp.int32, (tokens, span), 0)
    key_pos = first - 2 * block + lax.broadcasted_iota(jnp.int32, (tokens, span), 1)
    row_pos = first + lax.broadcasted_iota(jnp.int32, (tokens, 128), 0)
    begin = jnp.zeros((tokens, 128), jnp.int32)
    end = jnp.int32(0)
    for n in range(lengths_ref.shape[0]):
        end = end + lengths_ref[n]
        begin = jnp.where(row_pos >= end, end, begin)
    visible = (key_pos >= begin[:, :1]) & (key_pos <= query_pos)
    bias[...] = jnp.where(visible, 0.0, -1e30)

    factor = math.log2(math.e) / math.sqrt(HEAD_SIZE)
    pair = 2 if width % 2 == 0 else 1
    reading = pl.ds(pl.multiple_of(me * tokens, tokens), span)

    def compute(g):
        key_part = kv.at[g, 0]
        value_part = kv.at[g, 1]

        def heads_of(j, carry):
            at = (g * width + j * pair) * HEAD_SIZE
            columns = [
                pl.ds(pl.multiple_of(at + p * HEAD_SIZE, HEAD_SIZE), HEAD_SIZE) for p in range(pair)
            ]
            q = jnp.concatenate([q_ref[:, c] for c in columns], axis=0)
            scores = lax.dot_general(
                q, key_part[reading, :], (((1,), (1,)), ((), ())), preferred_element_type=jnp.float32
            )
            scores = scores.reshape(pair, tokens, span) + bias[...][None]
            scores = scores.reshape(pair * tokens, span)
            top = jnp.max(scores, axis=1, keepdims=True)
            weights = jnp.exp2((scores - top) * factor)
            total = jnp.sum(weights, axis=1, keepdims=True)
            summed = jnp.dot(
                weights.astype(jnp.bfloat16), value_part[reading, :],
                preferred_element_type=jnp.float32,
            )
            result = (summed / total).astype(out_ref.dtype)
            for p in range(pair):
                out_ref[:, columns[p]] = result[p * tokens:(p + 1) * tokens]
            return carry

        lax.fori_loop(0, width // pair, heads_of, 0)

    def step(t, carry):
        for distance in range(1, heads):
            @pl.when((t >= distance - 1) & (t < groups + distance - 1))
            def _():
                z_arrived(t - distance + 1, distance)

        for distance in range(heads):
            @pl.when((t >= distance) & (t < groups + distance))
            def _():
                for shard in (me - distance, me + distance) if distance else (me,):
                    @pl.when((shard >= 0) & (shard < heads))
                    def _():
                        y_arrived(t - distance, shard)

        @pl.when(t >= heads)
        def _():
            for shard in range(heads):
                x_copy(t - heads, shard).wait_recv()
            compute(t - heads)

        return carry

    lax.fori_loop(0, groups + heads, step, 0)

    def drain(g, carry):
        for way in (1, -1):
            @pl.when(has_next(way))
            def _():
                z_copy(g, me, way).wait_send()

                for distance in range(1, heads):
                    shard = me - way * distance

                    @pl.when((shard >= 0) & (shard < heads))
                    def _():
                        z_copy(g, shard, way).wait_send()

        for shard in range(heads):
            @pl.when(y_needed(shard))
            def _():
                y_copy(g, shard).wait_send()

            x_copy(g, shard).wait_send()
        return carry

    lax.fori_loop(0, groups, drain, 0)


def solution(mesh):
    heads, outers, inners = (mesh.shape[name] for name in ("head", "outer", "inner"))

    def per_device(query, keys, values, lengths):
        tokens = query.shape[0]
        groups = keys.shape[1] // HEAD_SIZE
        return pl.pallas_call(
            functools.partial(kernel, heads, outers, inners),
            out_shape=jax.ShapeDtypeStruct(query.shape, query.dtype),
            in_specs=[
                pl.BlockSpec(memory_space=pltpu.SMEM),
                pl.BlockSpec(memory_space=pltpu.VMEM),
                pl.BlockSpec(memory_space=pl.ANY),
                pl.BlockSpec(memory_space=pl.ANY),
            ],
            out_specs=pl.BlockSpec(memory_space=pltpu.VMEM),
            scratch_shapes=[
                pltpu.VMEM((groups, 2, 3 * heads * tokens, HEAD_SIZE), jnp.bfloat16),
                pltpu.VMEM((tokens, (2 * heads + 1) * tokens), jnp.float32),
                pltpu.SemaphoreType.DMA((2, groups)),
                pltpu.SemaphoreType.DMA((heads + 1, groups)),
                pltpu.SemaphoreType.DMA((heads, groups)),
                pltpu.SemaphoreType.DMA((heads, groups)),
                pltpu.SemaphoreType.DMA((heads, groups)),
                pltpu.SemaphoreType.DMA((heads, groups)),
                pltpu.SemaphoreType.DMA((heads, groups)),
            ],
            compiler_params=pltpu.CompilerParams(collective_id=0, has_side_effects=True),
        )(lengths, query, keys, values)

    rows = P(("outer", "inner", "head"), None)
    return jax.shard_map(
        per_device,
        mesh=mesh,
        in_specs=(rows, rows, rows, P()),
        out_specs=rows,
        check_vma=False,
    )
```

profile of v0, /device:TPU:0, one launch (start us, length us, event | category | flops | bytes accessed | tf_op | source)
XLA Modules:
  0.0 80.9 jit_solution(9195801266801615827)
XLA Ops:
  0.0 77.8 %shard_map.46 = bf16[128,8192]{1,0:T(8,128)(2,1)} custom-call(s32[8]{0:T(128)} %lengths_ref.1, bf16[128,8192]{1,0:T(8,128)(2,1)} %q_ref.1, bf16[128,1024]{1,0:T(8,128)(2,1)} %k_ref.1, bf16[128,1024]{1,0:T(8,128)(2,1)} %v_ref.1), custom_call_target="tpu_custom_call" | custom-call | tf_op jit(solution)/shard_map/pallas_call | solution.py:237
  77.8 3.1 %copy.6 = bf16[128,8192]{1,0:T(8,128)(2,1)} copy(bf16[128,8192]{1,0:T(8,128)(2,1)} %shard_map.46) | data formatting | bytes 4194304
where the time goes:
time: 81.1 us; the launch traced here: 80.9 us
  Pallas kernels  77.8 us (96%)
  local copies, waits for them, and re-layouts  3.1 us (4%)
    pallas_call x1, Pallas kernels, per_device(): pl.pallas_call(functools.partial(kernel, heads, outers, inners), out_shap...  77.8 us
    unnamed x1, local copies, waits for them, and re-layouts  3.1 us

commit v1 on v0

v1 whole, which is shorter than its diff:
```python
import functools
import math

import jax
import jax.numpy as jnp
from jax import lax
from jax.experimental import pallas as pl
from jax.experimental.pallas import tpu as pltpu
from jax.sharding import PartitionSpec as P

HEAD_SIZE = 128
MESH = pl.DeviceIdType.MESH
BOTH, KEY, VALUE = pl.ds(0, 2), pl.ds(0, 1), pl.ds(1, 1)

TIMES = {
    "x own": (-30.16, -10.38),
    "y own": (-93.89, 0.80),
    "z mate": (-51.39, 15.57),
    "z own": (-16.10, 15.74),
    "z1": (16.36, 9.42),
    "z2": (24.86, 12.85),
    "z3": (44.16, 11.37),
    "y0": (13.69, 1.81),
    "y1": (31.15, 9.42),
    "y2": (45.44, 12.20),
    "y3": (54.66, 11.66),
    "x0": (45.67, 11.75),
    "compute": (66.38, 11.77),
}


def order_of(heads, groups, period):
    steps = []
    for name, (first, later) in TIMES.items():
        for g in range(groups):
            at = first + later * g
            if name == "compute":
                steps += [(at + later * j / period, 0, name, g, j) for j in range(period)]
                continue

            steps.append((at, 1, name, g, 0))
            if name in ("z3", "y3"):
                steps += [(at, d, name[0] + str(d), g, 0) for d in range(4, heads)]

    slots = [[]]
    for _, _, name, g, j in sorted(steps, key=lambda step: step[:2]):
        if name != "compute":
            slots[-1].append((name, g))
            continue

        if j == 0:
            slots[-1].append(("ready", g))
        slots.append([])
    return slots


def kernel(
    heads, outers, inners, lengths_ref, q_hbm, k_ref, v_ref, out_hbm,
    q_ref, out_ref, kv, bias, q_sem, out_sem, own_sem,
    z_send, z_recv, on_send, y_send, y_recv, x_send, x_recv, pair_send, pair_recv,
):
    tokens = q_ref.shape[0]
    groups = k_ref.shape[1] // HEAD_SIZE
    width = q_ref.shape[1] // k_ref.shape[1]
    pair = 2 if width % 2 == 0 else 1
    period = width // pair
    block = heads * tokens
    contexts = outers * inners
    span = (2 * heads + 1) * tokens
    me = lax.axis_index("head")
    ctx = lax.axis_index("outer") * inners + lax.axis_index("inner")
    odd = lax.rem(ctx, 2)
    side = lax.rem(me, 2)
    mate = me + 1 - 2 * side

    def context(steps):
        at = lax.rem(ctx + steps + contexts, contexts)
        return {"outer": at // inners, "inner": lax.rem(at, inners)}

    partner = context(1 - 2 * odd)

    def shard_of(k):
        other = lax.rem(me // 2 + k // 2, heads // 2)
        return 2 * other + (side if k % 2 == 0 else 1 - side)

    shards = [shard_of(k) for k in range(heads)]
    distances = [jnp.abs(shard - me) for shard in shards]

    def rows(at, shard):
        return pl.ds(pl.multiple_of(at * block + shard * tokens, tokens), tokens)

    def part_of(k):
        return KEY if k == 1 else BOTH

    def own_copy(g, which):
        ref = (k_ref, v_ref)[which]
        return pltpu.make_async_copy(
            ref.at[:, pl.ds(pl.multiple_of(g * HEAD_SIZE, HEAD_SIZE), HEAD_SIZE)],
            kv.at[g, which, rows(2, me), :],
            own_sem.at[which, g],
        )

    def remote(g, part, source, landing, send, recv, place):
        return pltpu.make_async_remote_copy(
            src_ref=kv.at[g, part, source, :], dst_ref=kv.at[g, part, landing, :],
            send_sem=send, recv_sem=recv, device_id=place, device_id_type=MESH,
        )

    def z_own(g, k, part):
        at = rows(2, me)
        slot = (1 if k == 1 and part is VALUE else 0, k, g)
        recv = (1 if k == 1 and part is VALUE else 0, me, g)
        return remote(g, part, at, at, z_send.at[slot], z_recv.at[recv], {"head": shards[k]})

    def z_on(g, k):
        at = rows(2, shards[k])
        to = jnp.clip(me + jnp.where(shards[k] < me, 1, -1), 0, heads - 1)
        return remote(
            g, BOTH, at, at, on_send.at[k, g], z_recv.at[0, shards[k], g], {"head": to}
        )

    def z_goes_on(k):
        beyond = jnp.where(shards[k] < me, me + 1 < heads, me >= 1)
        return (distances[k] >= 2) & beyond

    def z_arrival(g, k, part):
        at = rows(2, shards[k])
        recv = (1 if k == 1 and part is VALUE else 0, shards[k], g)
        return remote(g, part, at, at, on_send.at[k, g], z_recv.at[recv], {"head": mate})

    def y_copy(g, k):
        return remote(
            g, part_of(k), rows(2, shards[k]), rows(0, shards[k]),
            y_send.at[k, g], y_recv.at[k, g], context(2),
        )

    def x_copy(g, k):
        return remote(
            g, part_of(k), rows(2 * (1 - odd), shards[k]), rows(1, shards[k]),
            x_send.at[k, g], x_recv.at[k, g], partner,
        )

    def pair_copy(g, at):
        return remote(
            g, VALUE, rows(at, me), rows(at, me), pair_send.at[at, g], pair_recv.at[at, g],
            {"head": mate},
        )

    def pair_arrival(g, at):
        return remote(
            g, VALUE, rows(at, mate), rows(at, mate), pair_send.at[at, g], pair_recv.at[at, g],
            {"head": mate},
        )

    def y_needed(k):
        return (odd == 1) | (shards[k] >= me)

    def have(g, k):
        @pl.when(y_needed(k))
        def _():
            y_copy(g, k).start()

        @pl.when(odd == 0)
        def _():
            x_copy(g, k).start()

    def x_own_event(g):
        @pl.when(odd == 0)
        def _():
            x_copy(g, 0).start()

    def y_own_event(g):
        y_copy(g, 0).start()

    def mate_event(g):
        @pl.when(side == 0)
        def _():
            z_own(g, 1, VALUE).start()

        z_own(g, 1, KEY).start()

    def z_own_event(g):
        for k in range(2, heads):
            @pl.when(distances[k] <= 2)
            def _():
                z_own(g, k, BOTH).start()

    def z_mate_event(g):
        z_arrival(g, 1, KEY).wait_recv()

        @pl.when(side == 1)
        def _():
            z_arrival(g, 1, VALUE).wait_recv()

        have(g, 1)

    def z_event(g, distance):
        for k in range(2, heads):
            @pl.when(jnp.maximum(distances[k], 2) == distance)
            def _():
                z_arrival(g, k, BOTH).wait_recv()

                @pl.when(z_goes_on(k))
                def _():
                    z_on(g, k).start()

                have(g, k)

    def y_step(g, k):
        @pl.when(y_needed(k))
        def _():
            y_copy(g, k).wait_recv()

        @pl.when(odd == 1)
        def _():
            x_copy(g, k).start()

        if k == 0:
            @pl.when(side == 1)
            def _():
                pair_copy(g, 0).start()

    def y_event(g, distance):
        for k in range(2, heads):
            @pl.when(jnp.maximum(distances[k], 2) == distance)
            def _():
                y_step(g, k)

    def x_event(g):
        x_copy(g, 0).wait_recv()
        pair_copy(g, 1).start()

    def final_event(g):
        for k in range(1, heads):
            x_copy(g, k).wait_recv()
        pair_arrival(g, 1).wait_recv()

        @pl.when(side == 0)
        def _():
            pair_arrival(g, 0).wait_recv()

    actions = {
        "x own": x_own_event, "y own": y_own_event, "z mate": mate_event, "z own": z_own_event,
        "z1": z_mate_event, "y0": functools.partial(y_step, k=0),
        "y1": functools.partial(y_step, k=1), "x0": x_event, "ready": final_event,
    }
    for distance in range(2, heads):
        actions["z" + str(distance)] = functools.partial(z_event, distance=distance)
        actions["y" + str(distance)] = functools.partial(y_event, distance=distance)

    slots = order_of(heads, groups, period)
    loads = list(dict.fromkeys(g for slot in slots for name, g in slot if "own" in name or "mate" in name))

    q_copy = pltpu.make_async_copy(q_hbm, q_ref, q_sem)
    for g in loads:
        own_copy(g, 0).start()
        own_copy(g, 1).start()
    q_copy.start()

    barrier = pltpu.get_barrier_semaphore()
    for distance in range(1, heads):
        pl.semaphore_signal(
            barrier, inc=1, device_id={"head": lax.rem(me + distance, heads)}, device_id_type=MESH
        )
    for place in (context(2), context(-2), partner):
        pl.semaphore_signal(barrier, inc=1, device_id=place, device_id_type=MESH)
    pl.semaphore_wait(barrier, heads - 1 + 3)

    def fill_bias():
        first = ctx * block + me * tokens
        query_pos = first + lax.broadcasted_iota(jnp.int32, (tokens, span), 0)
        key_pos = first - 2 * block + lax.broadcasted_iota(jnp.int32, (tokens, span), 1)
        row_pos = first + lax.broadcasted_iota(jnp.int32, (tokens, 128), 0)
        begin = jnp.zeros((tokens, 128), jnp.int32)
        end = jnp.int32(0)
        for n in range(lengths_ref.shape[0]):
            end = end + lengths_ref[n]
            begin = jnp.where(row_pos >= end, end, begin)
        visible = (key_pos >= begin[:, :1]) & (key_pos <= query_pos)
        bias[...] = jnp.where(visible, 0.0, -1e30)

    factor = math.log2(math.e) / math.sqrt(HEAD_SIZE)
    reading = pl.ds(pl.multiple_of(me * tokens, tokens), span)

    def out_copy(g):
        at = pl.ds(pl.multiple_of(g * width * HEAD_SIZE, HEAD_SIZE), width * HEAD_SIZE)
        return pltpu.make_async_copy(out_ref.at[:, at], out_hbm.at[:, at], out_sem.at[g])

    def compute(g, j):
        key_part = kv.at[g, 0]
        value_part = kv.at[g, 1]
        at = (g * width + j * pair) * HEAD_SIZE
        columns = [
            pl.ds(pl.multiple_of(at + p * HEAD_SIZE, HEAD_SIZE), HEAD_SIZE) for p in range(pair)
        ]
        q = jnp.concatenate([q_ref[:, c] for c in columns], axis=0)
        scores = lax.dot_general(
            q, key_part[reading, :], (((1,), (1,)), ((), ())), preferred_element_type=jnp.float32
        )
        scores = scores.reshape(pair, tokens, span) + bias[...][None]
        scores = scores.reshape(pair * tokens, span)
        top = jnp.max(scores, axis=1, keepdims=True)
        weights = jnp.exp2((scores - top) * factor)
        total = jnp.sum(weights, axis=1, keepdims=True)
        summed = jnp.dot(
            weights.astype(jnp.bfloat16), value_part[reading, :],
            preferred_element_type=jnp.float32,
        )
        result = (summed / total).astype(out_ref.dtype)
        for p in range(pair):
            out_ref[:, columns[p]] = result[p * tokens:(p + 1) * tokens]

    loaded = set()

    def take(slot):
        for name, g in slot:
            if g not in loaded:
                loaded.add(g)
                own_copy(g, 0).wait()
                own_copy(g, 1).wait()
            actions[name](g)

    def dispatch(step, low, high):
        if not any(slots[low:high]):
            return

        if high - low == 1:
            take(slots[low])
            return

        middle = (low + high) // 2

        @pl.when(step < middle)
        def _():
            dispatch(step, low, middle)

        @pl.when(step >= middle)
        def _():
            dispatch(step, middle, high)

    take(slots[0][:groups])
    fill_bias()
    take(slots[0][groups:])
    q_copy.wait()

    def group_step(g, carry):
        def head_step(j, carry):
            compute(g, j)
            dispatch(g * period + j + 1, 1, groups * period + 1)
            return carry

        lax.fori_loop(0, period, head_step, 0)
        out_copy(g).start()
        return carry

    lax.fori_loop(0, groups, group_step, 0)

    def drain(g, carry):
        z_own(g, 1, KEY).wait_send()

        @pl.when(side == 0)
        def _():
            z_own(g, 1, VALUE).wait_send()

        for k in range(2, heads):
            @pl.when(distances[k] <= 2)
            def _():
                z_own(g, k, BOTH).wait_send()

            @pl.when(z_goes_on(k))
            def _():
                z_on(g, k).wait_send()

        for k in range(heads):
            @pl.when(y_needed(k))
            def _():
                y_copy(g, k).wait_send()

            x_copy(g, k).wait_send()

        pair_copy(g, 1).wait_send()

        @pl.when(side == 1)
        def _():
            pair_copy(g, 0).wait_send()

        out_copy(g).wait()
        return carry

    lax.fori_loop(0, groups, drain, 0)


def solution(mesh):
    heads, outers, inners = (mesh.shape[name] for name in ("head", "outer", "inner"))

    def per_device(query, keys, values, lengths):
        tokens = query.shape[0]
        groups = keys.shape[1] // HEAD_SIZE
        sems = pltpu.SemaphoreType.DMA
        return pl.pallas_call(
            functools.partial(kernel, heads, outers, inners),
            out_shape=jax.ShapeDtypeStruct(query.shape, query.dtype),
            in_specs=[
                pl.BlockSpec(memory_space=pltpu.SMEM),
                pl.BlockSpec(memory_space=pl.ANY),
                pl.BlockSpec(memory_space=pl.ANY),
                pl.BlockSpec(memory_space=pl.ANY),
            ],
            out_specs=pl.BlockSpec(memory_space=pl.ANY),
            scratch_shapes=[
                pltpu.VMEM(query.shape, query.dtype),
                pltpu.VMEM(query.shape, query.dtype),
                pltpu.VMEM((groups, 2, 3 * heads * tokens, HEAD_SIZE), jnp.bfloat16),
                pltpu.VMEM((tokens, (2 * heads + 1) * tokens), jnp.float32),
                sems,
                sems((groups,)),
                sems((2, groups)),
                sems((2, heads, groups)),
                sems((2, heads, groups)),
                sems((heads, groups)),
                sems((heads, groups)),
                sems((heads, groups)),
                sems((heads, groups)),
                sems((heads, groups)),
                sems((2, groups)),
                sems((2, groups)),
            ],
            compiler_params=pltpu.CompilerParams(collective_id=0, has_side_effects=True),
        )(lengths, query, keys, values)

    rows = P(("outer", "inner", "head"), None)
    return jax.shard_map(
        per_device,
        mesh=mesh,
        in_specs=(rows, rows, rows, P()),
        out_specs=rows,
        check_vma=False,
    )
```

time: 81.1 us -> 70.1 us (0.86)
  Pallas kernels: 77.8 us -> 66.8 us
    pallas_call x1, Pallas kernels: 77.8 us -> 66.8 us  [per_device(): pl.pallas_call(functools.partial(kernel, heads, outers, inners), out_shap...]
where the time goes in v1:
time: 70.1 us; the launch traced here: 69.9 us
  Pallas kernels  66.8 us (95%)
  local copies, waits for them, and re-layouts  3.1 us (4%)
    pallas_call x1, Pallas kernels, per_device(): pl.pallas_call(functools.partial(kernel, heads, outers, inners), out_shap...  66.8 us
    unnamed x1, local copies, waits for them, and re-layouts  3.1 us

profile of v1, /device:TPU:0, one launch (start us, length us, event | category | flops | bytes accessed | tf_op | source)
XLA Modules:
  0.0 69.9 jit_solution(5526140823497745178)
XLA Ops:
  0.0 66.8 %shard_map.46 = bf16[128,8192]{1,0:T(8,128)(2,1)} custom-call(s32[8]{0:T(128)} %lengths_ref.1, bf16[128,8192]{1,0:T(8,128)(2,1)} %q_hbm.1, bf16[128,1024]{1,0:T(8,128)(2,1)} %k_ref.1, bf16[128,1024]{1,0:T(8,128)(2,1)} %v_ref.1), custom_call_target="tpu_custom_call" | custom-call | tf_op jit(solution)/shard_map/pallas_call | solution.py:400
  66.8 3.1 %copy.6 = bf16[128,8192]{1,0:T(8,128)(2,1)} copy(bf16[128,8192]{1,0:T(8,128)(2,1)} %shard_map.46) | data formatting | bytes 4194304

commit v2 on v1

--- a/solution.py
+++ b/solution.py
@@ -13,19 +13,19 @@
 BOTH, KEY, VALUE = pl.ds(0, 2), pl.ds(0, 1), pl.ds(1, 1)
 
 TIMES = {
-    "x own": (-30.16, -10.38),
-    "y own": (-93.89, 0.80),
-    "z mate": (-51.39, 15.57),
-    "z own": (-16.10, 15.74),
-    "z1": (16.36, 9.42),
-    "z2": (24.86, 12.85),
-    "z3": (44.16, 11.37),
-    "y0": (13.69, 1.81),
-    "y1": (31.15, 9.42),
-    "y2": (45.44, 12.20),
-    "y3": (54.66, 11.66),
-    "x0": (45.67, 11.75),
-    "compute": (66.38, 11.77),
+    "x own": (-0.79, -14.57),
+    "y own": (-250.76, 11.43),
+    "z mate": (-54.63, 3.55),
+    "z own": (-56.68, 24.08),
+    "z1": (-23.74, 8.00),
+    "z2": (13.60, 18.83),
+    "z3": (33.48, 17.76),
+    "y0": (-28.36, 8.15),
+    "y1": (15.77, 5.69),
+    "y2": (47.00, 17.93),
+    "y3": (57.14, 17.66),
+    "x0": (38.87, 20.69),
+    "compute": (77.81, 17.72),
 }
 
 
@@ -54,16 +54,21 @@
     return slots
 
 
+def pair_of(width):
+    return 2 if width % 8 == 0 else 1
+
+
 def kernel(
-    heads, outers, inners, lengths_ref, q_hbm, k_ref, v_ref, out_hbm,
-    q_ref, out_ref, kv, bias, q_sem, out_sem, own_sem,
+    heads, outers, inners, lengths_ref, q_hbm, k_ref, v_ref, out_ref,
+    q_ref, kv, bias, held, tops, totals, rounded, q_sem, own_sem,
     z_send, z_recv, on_send, y_send, y_recv, x_send, x_recv, pair_send, pair_recv,
 ):
     tokens = q_ref.shape[0]
     groups = k_ref.shape[1] // HEAD_SIZE
     width = q_ref.shape[1] // k_ref.shape[1]
-    pair = 2 if width % 2 == 0 else 1
+    pair = pair_of(width)
     period = width // pair
+    steps = groups * period
     block = heads * tokens
     contexts = outers * inners
     span = (2 * heads + 1) * tokens
@@ -282,33 +287,35 @@
     factor = math.log2(math.e) / math.sqrt(HEAD_SIZE)
     reading = pl.ds(pl.multiple_of(me * tokens, tokens), span)
 
-    def out_copy(g):
-        at = pl.ds(pl.multiple_of(g * width * HEAD_SIZE, HEAD_SIZE), width * HEAD_SIZE)
-        return pltpu.make_async_copy(out_ref.at[:, at], out_hbm.at[:, at], out_sem.at[g])
-
-    def compute(g, j):
-        key_part = kv.at[g, 0]
-        value_part = kv.at[g, 1]
-        at = (g * width + j * pair) * HEAD_SIZE
-        columns = [
+    def columns_of(n):
+        at = n * pair * HEAD_SIZE
+        return [
             pl.ds(pl.multiple_of(at + p * HEAD_SIZE, HEAD_SIZE), HEAD_SIZE) for p in range(pair)
         ]
-        q = jnp.concatenate([q_ref[:, c] for c in columns], axis=0)
+
+    def score(n, g, slot):
+        q = jnp.concatenate([q_ref[:, c] for c in columns_of(n)], axis=0)
         scores = lax.dot_general(
-            q, key_part[reading, :], (((1,), (1,)), ((), ())), preferred_element_type=jnp.float32
+            q, kv.at[g, 0][reading, :], (((1,), (1,)), ((), ())),
+            preferred_element_type=jnp.float32,
         )
         scores = scores.reshape(pair, tokens, span) + bias[...][None]
         scores = scores.reshape(pair * tokens, span)
-        top = jnp.max(scores, axis=1, keepdims=True)
-        weights = jnp.exp2((scores - top) * factor)
-        total = jnp.sum(weights, axis=1, keepdims=True)
+        held[slot][...] = scores
+        tops[slot][...] = jnp.max(scores, axis=1, keepdims=True)
+
+    def weigh(slot):
+        weights = jnp.exp2((held[slot][...] - tops[slot][...]) * factor)
+        totals[slot][...] = jnp.sum(weights, axis=1, keepdims=True)
+        rounded[slot][...] = weights.astype(jnp.bfloat16)
+
+    def attend(n, g, slot):
         summed = jnp.dot(
-            weights.astype(jnp.bfloat16), value_part[reading, :],
-            preferred_element_type=jnp.float32,
-        )
-        result = (summed / total).astype(out_ref.dtype)
-        for p in range(pair):
-            out_ref[:, columns[p]] = result[p * tokens:(p + 1) * tokens]
+            rounded[slot][...], kv.at[g, 1][reading, :], preferred_element_type=jnp.float32
+        )
+        result = (summed / totals[slot][...]).astype(out_ref.dtype)
+        for p, c in enumerate(columns_of(n)):
+            out_ref[:, c] = result[p * tokens:(p + 1) * tokens]
 
     loaded = set()
 
@@ -343,17 +350,29 @@
     take(slots[0][groups:])
     q_copy.wait()
 
+    held[1][...] = jnp.zeros_like(held[1])
+    tops[1][...] = jnp.zeros_like(tops[1])
+    for slot in range(2):
+        totals[slot][...] = jnp.ones_like(totals[slot])
+        rounded[slot][...] = jnp.zeros_like(rounded[slot])
+
     def group_step(g, carry):
-        def head_step(j, carry):
-            compute(g, j)
-            dispatch(g * period + j + 1, 1, groups * period + 1)
+        def two_steps(i, carry):
+            for slot in range(2):
+                n = g * period + 2 * i + slot
+                attend(jnp.maximum(n - 2, 0), jnp.maximum(jnp.where(i > 0, g, g - 1), 0), slot)
+                weigh(1 - slot)
+                score(n, g, slot)
+                dispatch(n + 1, 1, steps + 1)
             return carry
 
-        lax.fori_loop(0, period, head_step, 0)
-        out_copy(g).start()
+        lax.fori_loop(0, period // 2, two_steps, 0)
         return carry
 
     lax.fori_loop(0, groups, group_step, 0)
+    attend(steps - 2, groups - 1, 0)
+    weigh(1)
+    attend(steps - 1, groups - 1, 1)
 
     def drain(g, carry):
         z_own(g, 1, KEY).wait_send()
@@ -384,7 +403,6 @@
         def _():
             pair_copy(g, 0).wait_send()
 
-        out_copy(g).wait()
         return carry
 
     lax.fori_loop(0, groups, drain, 0)
@@ -397,23 +415,26 @@
         tokens = query.shape[0]
         groups = keys.shape[1] // HEAD_SIZE
         sems = pltpu.SemaphoreType.DMA
+        rows = pair_of(query.shape[1] // keys.shape[1]) * tokens
         return pl.pallas_call(
             functools.partial(kernel, heads, outers, inners),
-            out_shape=jax.ShapeDtypeStruct(query.shape, query.dtype),
+            out_shape=pltpu.VMEM(query.shape, query.dtype),
             in_specs=[
                 pl.BlockSpec(memory_space=pltpu.SMEM),
                 pl.BlockSpec(memory_space=pl.ANY),
                 pl.BlockSpec(memory_space=pl.ANY),
                 pl.BlockSpec(memory_space=pl.ANY),
             ],
-            out_specs=pl.BlockSpec(memory_space=pl.ANY),
+            out_specs=pl.BlockSpec(memory_space=pltpu.VMEM),
             scratch_shapes=[
-                pltpu.VMEM(query.shape, query.dtype),
                 pltpu.VMEM(query.shape, query.dtype),
                 pltpu.VMEM((groups, 2, 3 * heads * tokens, HEAD_SIZE), jnp.bfloat16),
                 pltpu.VMEM((tokens, (2 * heads + 1) * tokens), jnp.float32),
+                [pltpu.VMEM((rows, (2 * heads + 1) * tokens), jnp.float32)] * 2,
+                [pltpu.VMEM((rows, 1), jnp.float32)] * 2,
+                [pltpu.VMEM((rows, 1), jnp.float32)] * 2,
+                [pltpu.VMEM((rows, (2 * heads + 1) * tokens), jnp.bfloat16)] * 2,
                 sems,
-                sems((groups,)),
                 sems((2, groups)),
                 sems((2, heads, groups)),
                 sems((2, heads, groups)),

time: 70.1 us -> 63.4 us (0.904)
  Pallas kernels: 66.8 us -> 61.3 us
  local copies, waits for them, and re-layouts: 3.1 us -> 1.32 us
    pallas_call x1, Pallas kernels: 66.8 us -> 61.3 us  [per_device(): pl.pallas_call(functools.partial(kernel, heads, outers, inners), out_shap...]
    unnamed x1, local copies, waits for them, and re-layouts: 3.1 us -> 1.32 us
where the time goes in v2:
time: 63.4 us; the launch traced here: 62.6 us
  Pallas kernels  61.3 us (97%)
  local copies, waits for them, and re-layouts  1.32 us (2%)
    pallas_call x1, Pallas kernels, per_device(): pl.pallas_call(functools.partial(kernel, heads, outers, inners), out_shap...  61.3 us
    unnamed x1, local copies, waits for them, and re-layouts  1.32 us

profile of v2, /device:TPU:0, one launch (start us, length us, event | category | flops | bytes accessed | tf_op | source)
XLA Modules:
  0.0 62.6 jit_solution(7419382399646985394)
XLA Ops:
  0.0 61.3 %shard_map.46 = bf16[128,8192]{1,0:T(8,128)(2,1)S(1)} custom-call(s32[8]{0:T(128)} %lengths_ref.1, bf16[128,8192]{1,0:T(8,128)(2,1)} %q_hbm.1, bf16[128,1024]{1,0:T(8,128)(2,1)} %k_ref.1, bf16[128,1024]{1,0:T(8,128)(2,1)} %v_ref.1), custom_call_target="tpu_custom_call" | custom-call | tf_op jit(solution)/shard_map/pallas_call | solution.py:419
  61.3 1.3 %copy.6 = bf16[128,8192]{1,0:T(8,128)(2,1)} copy(bf16[128,8192]{1,0:T(8,128)(2,1)S(1)} %shard_map.46) | data formatting | bytes 4194304

commit v3 on v2

--- a/solution.py
+++ b/solution.py
@@ -13,20 +13,28 @@
 BOTH, KEY, VALUE = pl.ds(0, 2), pl.ds(0, 1), pl.ds(1, 1)
 
 TIMES = {
-    "x own": (-0.79, -14.57),
-    "y own": (-250.76, 11.43),
-    "z mate": (-54.63, 3.55),
-    "z own": (-56.68, 24.08),
-    "z1": (-23.74, 8.00),
-    "z2": (13.60, 18.83),
-    "z3": (33.48, 17.76),
-    "y0": (-28.36, 8.15),
-    "y1": (15.77, 5.69),
-    "y2": (47.00, 17.93),
-    "y3": (57.14, 17.66),
-    "x0": (38.87, 20.69),
-    "compute": (77.81, 17.72),
+    "x own": (-719.83, -349.03),
+    "y own": (-829.62, -84.81),
+    "z mate": (-730.34, 100.70),
+    "z own": (-775.75, 227.04),
+    "z1": (-281.24, 103.06),
+    "z2": (-53.00, 166.50),
+    "z3": (281.86, 145.34),
+    "y0": (-88.19, -49.55),
+    "y1": (-19.53, 92.10),
+    "y2": (348.49, 147.21),
+    "y3": (441.94, 155.24),
+    "x0": (306.38, 162.83),
+    "compute": (656.39, 147.59),
+    "z values": (-730.34, 100.70),
+    "pair": (-88.19, -49.55),
+    "z own odd": (-775.75, 227.04),
+    "z2 odd": (-53.00, 166.50),
+    "y2 odd": (348.49, 147.21),
 }
+
+
+OWN = ("x own", "y own", "z mate", "z values", "z own", "z own odd")
 
 
 def order_of(heads, groups, period):
@@ -34,11 +42,14 @@
     for name, (first, later) in TIMES.items():
         for g in range(groups):
             at = first + later * g
+            at = min(at, TIMES["compute"][0] + TIMES["compute"][1] * g - (name != "compute"))
             if name == "compute":
                 steps += [(at + later * j / period, 0, name, g, j) for j in range(period)]
                 continue
 
-            steps.append((at, 1, name, g, 0))
+            if name == "pair":
+                at = max(at, TIMES["y0"][0] + TIMES["y0"][1] * g)
+            steps.append((at, 2 if name == "pair" else 1, name, g, 0))
             if name in ("z3", "y3"):
                 steps += [(at, d, name[0] + str(d), g, 0) for d in range(4, heads)]
 
@@ -50,6 +61,8 @@
 
         if j == 0:
             slots[-1].append(("ready", g))
+        if j == 1 and g > 1:
+            slots[-1].append(("drain", g - 2))
         slots.append([])
     return slots
 
@@ -60,7 +73,7 @@
 
 def kernel(
     heads, outers, inners, lengths_ref, q_hbm, k_ref, v_ref, out_ref,
-    q_ref, kv, bias, held, tops, totals, rounded, q_sem, own_sem,
+    q_ref, kv, bias, own_doc, other_doc, held, tops, totals, rounded, q_sem, own_sem,
     z_send, z_recv, on_send, y_send, y_recv, x_send, x_recv, pair_send, pair_recv,
 ):
     tokens = q_ref.shape[0]
@@ -178,29 +191,30 @@
         y_copy(g, 0).start()
 
     def mate_event(g):
+        z_own(g, 1, KEY).start()
+
+    def mate_values_event(g):
         @pl.when(side == 0)
         def _():
             z_own(g, 1, VALUE).start()
 
-        z_own(g, 1, KEY).start()
-
-    def z_own_event(g):
-        for k in range(2, heads):
+    def pair_event(g):
+        @pl.when(side == 1)
+        def _():
+            pair_copy(g, 0).start()
+
+    def z_own_event(g, first):
+        for k in range(first, heads, 2):
             @pl.when(distances[k] <= 2)
             def _():
                 z_own(g, k, BOTH).start()
 
     def z_mate_event(g):
         z_arrival(g, 1, KEY).wait_recv()
-
-        @pl.when(side == 1)
-        def _():
-            z_arrival(g, 1, VALUE).wait_recv()
-
         have(g, 1)
 
-    def z_event(g, distance):
-        for k in range(2, heads):
+    def z_event(g, distance, which):
+        for k in which:
             @pl.when(jnp.maximum(distances[k], 2) == distance)
             def _():
                 z_arrival(g, k, BOTH).wait_recv()
@@ -220,13 +234,8 @@
         def _():
             x_copy(g, k).start()
 
-        if k == 0:
-            @pl.when(side == 1)
-            def _():
-                pair_copy(g, 0).start()
-
-    def y_event(g, distance):
-        for k in range(2, heads):
+    def y_event(g, distance, which):
+        for k in which:
             @pl.when(jnp.maximum(distances[k], 2) == distance)
             def _():
                 y_step(g, k)
@@ -244,17 +253,61 @@
         def _():
             pair_arrival(g, 0).wait_recv()
 
+        @pl.when(side == 1)
+        def _():
+            z_arrival(g, 1, VALUE).wait_recv()
+
+    def drain(g, carry):
+        z_own(g, 1, KEY).wait_send()
+
+        @pl.when(side == 0)
+        def _():
+            z_own(g, 1, VALUE).wait_send()
+
+        for k in range(2, heads):
+            @pl.when(distances[k] <= 2)
+            def _():
+                z_own(g, k, BOTH).wait_send()
+
+            @pl.when(z_goes_on(k))
+            def _():
+                z_on(g, k).wait_send()
+
+        for k in range(heads):
+            @pl.when(y_needed(k))
+            def _():
+                y_copy(g, k).wait_send()
+
+            x_copy(g, k).wait_send()
+
+        pair_copy(g, 1).wait_send()
+
+        @pl.when(side == 1)
+        def _():
+            pair_copy(g, 0).wait_send()
+
+        return carry
+
     actions = {
-        "x own": x_own_event, "y own": y_own_event, "z mate": mate_event, "z own": z_own_event,
+        "x own": x_own_event, "y own": y_own_event, "z mate": mate_event,
+        "z values": mate_values_event, "pair": pair_event,
+        "z own": functools.partial(z_own_event, first=2),
+        "z own odd": functools.partial(z_own_event, first=3),
         "z1": z_mate_event, "y0": functools.partial(y_step, k=0),
         "y1": functools.partial(y_step, k=1), "x0": x_event, "ready": final_event,
+        "drain": lambda g: drain(g, 0),
     }
-    for distance in range(2, heads):
-        actions["z" + str(distance)] = functools.partial(z_event, distance=distance)
-        actions["y" + str(distance)] = functools.partial(y_event, distance=distance)
+    even, uneven = range(2, heads, 2), range(3, heads, 2)
+    for axis, event in (("z", z_event), ("y", y_event)):
+        actions[axis + "2"] = functools.partial(event, distance=2, which=even)
+        actions[axis + "2 odd"] = functools.partial(event, distance=2, which=uneven)
+        for distance in range(3, heads):
+            actions[axis + str(distance)] = functools.partial(
+                event, distance=distance, which=range(2, heads)
+            )
 
     slots = order_of(heads, groups, period)
-    loads = list(dict.fromkeys(g for slot in slots for name, g in slot if "own" in name or "mate" in name))
+    loads = list(dict.fromkeys(g for slot in slots for name, g in slot if name in OWN))
 
     q_copy = pltpu.make_async_copy(q_hbm, q_ref, q_sem)
     for g in loads:
@@ -271,18 +324,28 @@
         pl.semaphore_signal(barrier, inc=1, device_id=place, device_id_type=MESH)
     pl.semaphore_wait(barrier, heads - 1 + 3)
 
-    def fill_bias():
-        first = ctx * block + me * tokens
-        query_pos = first + lax.broadcasted_iota(jnp.int32, (tokens, span), 0)
-        key_pos = first - 2 * block + lax.broadcasted_iota(jnp.int32, (tokens, span), 1)
-        row_pos = first + lax.broadcasted_iota(jnp.int32, (tokens, 128), 0)
-        begin = jnp.zeros((tokens, 128), jnp.int32)
+    def documents(positions, lanes):
+        number = jnp.zeros(positions.shape, jnp.int32)
         end = jnp.int32(0)
         for n in range(lengths_ref.shape[0]):
             end = end + lengths_ref[n]
-            begin = jnp.where(row_pos >= end, end, begin)
-        visible = (key_pos >= begin[:, :1]) & (key_pos <= query_pos)
-        bias[...] = jnp.where(visible, 0.0, -1e30)
+            number = number + (positions >= end).astype(jnp.int32)
+        return (number == lanes) & (positions >= 0)
+
+    def fill_masks():
+        first = ctx * block + me * tokens
+        shape = (tokens, HEAD_SIZE)
+        row = lax.broadcasted_iota(jnp.int32, shape, 0)
+        lanes = lax.broadcasted_iota(jnp.int32, shape, 1)
+        same = jnp.where(documents(first + row, lanes), 1.0, 0.0).astype(jnp.bfloat16)
+        for p in range(pair):
+            own_doc[p * tokens:(p + 1) * tokens, :] = same
+        for n in range(2 * heads + 1):
+            seen = documents(first - 2 * block + n * tokens + row, lanes)
+            other_doc[n * tokens:(n + 1) * tokens, :] = jnp.where(seen, 0.0, -1e30).astype(jnp.bfloat16)
+        shape = (tokens, tokens)
+        later = lax.broadcasted_iota(jnp.int32, shape, 1) > lax.broadcasted_iota(jnp.int32, shape, 0)
+        bias[...] = jnp.where(later, -1e30, 0.0)
 
     factor = math.log2(math.e) / math.sqrt(HEAD_SIZE)
     reading = pl.ds(pl.multiple_of(me * tokens, tokens), span)
@@ -295,14 +358,19 @@
 
     def score(n, g, slot):
         q = jnp.concatenate([q_ref[:, c] for c in columns_of(n)], axis=0)
+        q = jnp.concatenate([q, own_doc[...]], axis=1)
+        key = jnp.concatenate([kv.at[g, 0][reading, :], other_doc[...]], axis=1)
         scores = lax.dot_general(
-            q, kv.at[g, 0][reading, :], (((1,), (1,)), ((), ())),
-            preferred_element_type=jnp.float32,
-        )
-        scores = scores.reshape(pair, tokens, span) + bias[...][None]
-        scores = scores.reshape(pair * tokens, span)
-        held[slot][...] = scores
-        tops[slot][...] = jnp.max(scores, axis=1, keepdims=True)
+            q, key, (((1,), (1,)), ((), ())), preferred_element_type=jnp.float32
+        )
+        earlier = scores[:, :span - tokens]
+        recent = scores[:, span - tokens:].reshape(pair, tokens, tokens) + bias[...][None]
+        recent = recent.reshape(pair * tokens, tokens)
+        held[slot][:, :span - tokens] = earlier
+        held[slot][:, span - tokens:] = recent
+        tops[slot][...] = jnp.maximum(
+            jnp.max(earlier, axis=1, keepdims=True), jnp.max(recent, axis=1, keepdims=True)
+        )
 
     def weigh(slot):
         weights = jnp.exp2((held[slot][...] - tops[slot][...]) * factor)
@@ -346,7 +414,7 @@
             dispatch(step, middle, high)
 
     take(slots[0][:groups])
-    fill_bias()
+    fill_masks()
     take(slots[0][groups:])
     q_copy.wait()
 
@@ -360,9 +428,9 @@
         def two_steps(i, carry):
             for slot in range(2):
                 n = g * period + 2 * i + slot
+                score(n, g, slot)
+                weigh(1 - slot)
                 attend(jnp.maximum(n - 2, 0), jnp.maximum(jnp.where(i > 0, g, g - 1), 0), slot)
-                weigh(1 - slot)
-                score(n, g, slot)
                 dispatch(n + 1, 1, steps + 1)
             return carry
 
@@ -374,38 +442,7 @@
     weigh(1)
     attend(steps - 1, groups - 1, 1)
 
-    def drain(g, carry):
-        z_own(g, 1, KEY).wait_send()
-
-        @pl.when(side == 0)
-        def _():
-            z_own(g, 1, VALUE).wait_send()
-
-        for k in range(2, heads):
-            @pl.when(distances[k] <= 2)
-            def _():
-                z_own(g, k, BOTH).wait_send()
-
-            @pl.when(z_goes_on(k))
-            def _():
-                z_on(g, k).wait_send()
-
-        for k in range(heads):
-            @pl.when(y_needed(k))
-            def _():
-                y_copy(g, k).wait_send()
-
-            x_copy(g, k).wait_send()
-
-        pair_copy(g, 1).wait_send()
-
-        @pl.when(side == 1)
-        def _():
-            pair_copy(g, 0).wait_send()
-
-        return carry
-
-    lax.fori_loop(0, groups, drain, 0)
+    lax.fori_loop(max(groups - 2, 0), groups, drain, 0)
 
 
 def solution(mesh):
@@ -429,7 +466,9 @@
             scratch_shapes=[
                 pltpu.VMEM(query.shape, query.dtype),
                 pltpu.VMEM((groups, 2, 3 * heads * tokens, HEAD_SIZE), jnp.bfloat16),
-                pltpu.VMEM((tokens, (2 * heads + 1) * tokens), jnp.float32),
+                pltpu.VMEM((tokens, tokens), jnp.float32),
+                pltpu.VMEM((rows, HEAD_SIZE), jnp.bfloat16),
+                pltpu.VMEM(((2 * heads + 1) * tokens, HEAD_SIZE), jnp.bfloat16),
                 [pltpu.VMEM((rows, (2 * heads + 1) * tokens), jnp.float32)] * 2,
                 [pltpu.VMEM((rows, 1), jnp.float32)] * 2,
                 [pltpu.VMEM((rows, 1), jnp.float32)] * 2,

time: 63.4 us -> 62.7 us (0.989)
  no operation moved by 1% of the time
where the time goes in v3:
time: 62.7 us; the launch traced here: 62.5 us
  Pallas kernels  61.2 us (98%)
  local copies, waits for them, and re-layouts  1.32 us (2%)
    pallas_call x1, Pallas kernels, per_device(): pl.pallas_call(functools.partial(kernel, heads, outers, inners), out_shap...  61.2 us
    unnamed x1, local copies, waits for them, and re-layouts  1.32 us

profile of v3, /device:TPU:0, one launch (start us, length us, event | category | flops | bytes accessed | tf_op | source)
XLA Modules:
  0.0 62.5 jit_solution(5471541404533109935)
XLA Ops:
  0.0 61.2 %shard_map.46 = bf16[128,8192]{1,0:T(8,128)(2,1)S(1)} custom-call(s32[8]{0:T(128)} %lengths_ref.1, bf16[128,8192]{1,0:T(8,128)(2,1)} %q_hbm.1, bf16[128,1024]{1,0:T(8,128)(2,1)} %k_ref.1, bf16[128,1024]{1,0:T(8,128)(2,1)} %v_ref.1), custom_call_target="tpu_custom_call" | custom-call | tf_op jit(solution)/shard_map/pallas_call | solution.py:456
  61.2 1.3 %copy.6 = bf16[128,8192]{1,0:T(8,128)(2,1)} copy(bf16[128,8192]{1,0:T(8,128)(2,1)S(1)} %shard_map.46) | data formatting | bytes 4194304
